TPU v7x, 32 devices: a whole 2x2x4 slice. The times are simulated.
32 devices in a mesh: band: 4 (over y, core), col: 8 (over z, x).
Axes of the slice: x: 2, y: 2, z: 4, core: 2. Of those that a mesh axis runs over, the one named last changes fastest.
Arguments:
- source: bfloat16 [6, 524288], P(None, ('band', 'col')), may hold values from -6 to 6
- weights: bfloat16 [8192, 128, 128], P(('band', 'col')), may hold values from -0.5 to 0.5
- source_block: int32 [8192], P(('band', 'col')), may hold values from 0 to 127
- owner_device: int32 [8192, 1], P(('band', 'col')), may hold values from 0 to 31, as said below
- target_tile: int32 [8192], P(('band', 'col')), may hold values from 0 to 112, as said below
- cutoff: int32 [64], P(('band', 'col')), may hold values from 1 to 511
Outputs:
- remapped: float32 [6, 64, 7200], P(None, 'band', 'col')
- filtered: float32 [6, 64, 7200], P(None, 'band', 'col')
Inputs may be any that keep to these rules, and one draw needn't show every extreme that they name: `owner_device`: owners are numbered band index times 8 plus col index. A device's blocks go only to owners in its own band or in the bands next to it. Among the 256 blocks of one device at most 24 share an owner; in every device exactly 24 do for some owner of its own band, and exactly 24 for some owner of each band next to its own; every device sends at least 15 blocks to each owner of its own band. `target_tile`: every tile of every owner receives at least one block.
All inputs are finite; a program needn't handle non-finite values.
Results may differ from a plain program's by a relative error of at most 0.0003.
Values sent between devices are 32-bit elements; how exact they have to be, the bound alone decides.
A program may use at most 64 MiB of HBM per device.

v0:
```python
import jax
import jax.numpy as jnp
from jax import lax
from jax.sharding import PartitionSpec as P

NLON = 7200
KW = 512
TWO_PI = 6.283185307179586


def extended(array, sides, width):
    for axis, dim in sides:
        size, length = (lax.axis_size(axis), array.shape[dim])
        up = [(i, (i + 1) % size) for i in range(size - 1)]
        down = [(j, i) for i, j in up]
        last = lax.slice_in_dim(array, length - width, length, axis=dim)
        leading = lax.slice_in_dim(array, 0, width, axis=dim)
        before = lax.ppermute(last, axis, up)
        after = lax.ppermute(leading, axis, down)
        array = jnp.concatenate([before, array, after], axis=dim)
    return array


def zonal_table(start_index, length, period, wave_count):
    positions = start_index + lax.broadcasted_iota(jnp.int32, (length, wave_count), 0)
    wave_index = lax.broadcasted_iota(jnp.int32, (length, wave_count), 1)
    phases = positions * wave_index % period
    angles = phases.astype(jnp.float32) * (TWO_PI / period)
    return jnp.concatenate([jnp.cos(angles), jnp.sin(angles)], axis=1)


def spectral_weights(cutoffs, wave_count, period):
    wave_index = lax.broadcasted_iota(jnp.int32, (cutoffs.shape[0], wave_count), 1)
    scaled = jnp.where(wave_index == 0, 1.0, 2.0) / period
    retained = jnp.where(wave_index <= cutoffs[:, None], scaled, 0.0).astype(jnp.float32)
    return jnp.concatenate([retained, retained], axis=1)


def local(source, weights, source_block, owner_device, target_tile, cutoff):
    col_count = lax.axis_size("col")
    levels = source.shape[0]
    block_count = weights.shape[0]
    block_width = weights.shape[1]
    lat_here = cutoff.shape[0]
    lat_band = lat_here * col_count
    longitudes_here = NLON // col_count
    cell_count = lat_band * longitudes_here
    tile_count = (cell_count + block_width - 1) // block_width
    regular = (tile_count + col_count - 1) // col_count
    capacity = regular + max(
        1, (block_count - col_count * regular + 2 * col_count - 1) // (2 * col_count)
    )
    slot_total = 3 * col_count * capacity
    blocks_here = source.reshape(levels, -1, block_width)
    picked = jnp.take(blocks_here, source_block, axis=1)
    partial_value = jnp.einsum("lnb,nbt->nlt", picked, weights, preferred_element_type=jnp.float32)
    tile_rows = jnp.broadcast_to(
        target_tile.astype(jnp.float32)[:, None, None], (block_count, 1, block_width)
    )
    tagged = jnp.concatenate([partial_value, tile_rows], axis=1)
    owners = owner_device[:, 0]
    owner_band = owners // col_count
    owner_col = owners % col_count
    offset = owner_band - lax.axis_index("band") + 1
    row_index = lax.broadcasted_iota(jnp.int32, (block_count, block_count), 0)
    column_index = lax.broadcasted_iota(jnp.int32, (block_count, block_count), 1)
    earlier = (owners[None, :] == owners[:, None]) & (column_index < row_index)
    rank_within = jnp.sum(earlier.astype(jnp.int32), axis=1)
    slot_index = (offset * col_count + owner_col) * capacity + rank_within
    placing = lax.broadcasted_iota(jnp.int32, (slot_total, block_count), 0) == slot_index[None, :]
    outgoing = jnp.dot(
        placing.astype(jnp.float32),
        tagged.reshape(block_count, (levels + 1) * block_width),
        precision=lax.Precision.HIGHEST,
        preferred_element_type=jnp.float32,
    )
    outgoing = outgoing.reshape(3, col_count, capacity, levels + 1, block_width)
    rimmed = extended(jnp.stack([outgoing[0], outgoing[2]]), (("band", 0),), 1)
    arranged = jnp.stack([rimmed[0], outgoing[1], rimmed[3]])
    received = lax.all_to_all(arranged, "col", split_axis=1, concat_axis=1, tiled=True)
    slot_rows = received.reshape(-1, levels + 1, block_width)
    slot_owned = slot_rows[:, levels, 0].astype(jnp.int32)
    slot_data = slot_rows[:, :levels, :].reshape(-1, levels * block_width)
    chooser = (
        lax.broadcasted_iota(jnp.int32, (tile_count, slot_owned.shape[0]), 0) == slot_owned[None, :]
    ).astype(jnp.float32)
    summed = jnp.dot(
        chooser, slot_data, precision=lax.Precision.HIGHEST, preferred_element_type=jnp.float32
    )
    summed = jnp.transpose(summed.reshape(tile_count, levels, block_width), (1, 0, 2)).reshape(
        levels, tile_count * block_width
    )
    remapped = summed[:, :cell_count].reshape(levels, lat_band, longitudes_here)
    retained = spectral_weights(cutoff, KW, NLON)
    local_table = zonal_table(lax.axis_index("col") * longitudes_here, longitudes_here, NLON, KW)
    partial_spectra = jnp.dot(
        remapped.reshape(levels * lat_band, longitudes_here),
        local_table,
        precision=lax.Precision.HIGHEST,
        preferred_element_type=jnp.float32,
    )
    partial_spectra = partial_spectra.reshape(levels, lat_band, 2 * KW)
    spectrum = lax.psum_scatter(partial_spectra, "col", scatter_dimension=1, tiled=True)
    spectrum = spectrum * retained[None]
    band_spectra = lax.all_gather(spectrum, "col", axis=1, tiled=True)
    filtered = jnp.dot(
        band_spectra.reshape(levels * lat_band, 2 * KW),
        local_table.T,
        precision=lax.Precision.HIGHEST,
        preferred_element_type=jnp.float32,
    )
    filtered = filtered.reshape(levels, lat_band, longitudes_here)
    return (remapped, filtered)


def solution(mesh):
    in_specs = (
        P(None, ("band", "col")),
        P(("band", "col"), None, None),
        P(("band", "col")),
        P(("band", "col"), None),
        P(("band", "col")),
        P(("band", "col")),
    )
    out_specs = (P(None, "band", "col"), P(None, "band", "col"))
    return jax.shard_map(local, mesh=mesh, in_specs=in_specs, out_specs=out_specs, check_vma=False)
```

profile of v0, /device:TPU:0, one launch (start us, length us, event | category | flops | bytes accessed | tf_op | source)
XLA Modules:
  0.0 208.3 jit_solution(2805658013106343612)
XLA Ops:
  7.2 0.0 copy-start
  7.2 0.7 compare_and_fusion
  7.9 0.7 compare_select_fusion.1
  8.6 0.9 convert_reduce_fusion
  9.5 0.7 convert_element_type.22
  10.2 0.0 copy-done
  10.2 0.8 gather_fusion
  11.0 4.7 %fusion.12 = f32[256,6,128]{2,1,0:T(8,128)S(1)} fusion(bf16[256,128,128]{2,1,0:T(8,128)(2,1)} %param.7, bf16[256,6,128]{2,1,0:T(8,128)(2,1)S(1)} %gather_fusion, pred[256]{0:T(512)(128)(4,1)S(1)} %compare_and_fusion), kind=kOutput, calls=%fused_computation.20 | convolution fusion | flops 50528256 | bytes 9568512 | tf_op jit(solution)/shard_map/lnb,nbt->nlt/dot_general | solution.py:56
  15.8 0.3 broadcast_in_dim.37
  16.1 0.0 copy-start.2
  16.1 0.2 pad_maximum_fusion.1
  16.4 0.4 copy.32
  16.7 0.1 copy-done.2
  16.8 1.2 fusion.11
  18.0 0.1 fusion.29
  18.2 0.1 slice.28
  18.3 0.1 copy.33
  18.4 3.3 %collective-permute-start = (f32[1,8,24,7,128]{4,2,3,1,0:T(8,128)S(1)}, f32[1,8,24,7,128]{4,2,3,1,0:T(8,128)}, u32[]{:S(2)}, u32[]{:S(2)}) collective-permute-start(f32[1,8,24,7,128]{4,2,3,1,0:T(8,128)S(1)} %copy.33), channel_id=1, source_target_pairs={{0,8},{8,16},{16,24},{1,9},{9,17},{17,25},{2,10},{10,18},{18,26},{... | collective-permute-start | bytes 2064392 | tf_op jit(solution)/shard_map/ppermute | solution.py:18
  21.7 0.1 slice.32
  21.8 0.1 copy.34
  21.9 1.3 collective-permute-start.1
  23.2 0.1 slice.30
  23.3 0.0 collective-permute-done
  23.3 1.2 copy.35
  24.6 2.8 %collective-permute-done.1 = f32[1,8,24,7,128]{4,2,3,1,0:T(8,128)} collective-permute-done((f32[1,8,24,7,128]{4,2,3,1,0:T(8,128)S(1)}, f32[1,8,24,7,128]{4,2,3,1,0:T(8,128)}, u32[]{:S(2)}, u32[]{:S(2)}) %collective-permute-start.1) | collective-permute-done | bytes 688160 | tf_op jit(solution)/shard_map/ppermute | solution.py:19
  27.4 1.2 copy.36
  28.6 0.2 pad_maximum_fusion
  28.9 1.7 copy.37
  30.5 0.0 copy-start.4
  30.5 5.9 %all-to-all-start = ((f32[3,8,24,7,128]{4,2,3,0,1:T(8,128)}), f32[3,8,24,7,128]{4,2,3,0,1:T(8,128)}, u32[]{:S(2)}, u32[]{:S(2)}) async-start(f32[3,8,24,7,128]{4,2,3,0,1:T(8,128)} %copy.37), calls=%async_computation | async-start | bytes 4128768 | tf_op jit(solution)/shard_map/all_to_all | solution.py:80
  36.4 0.0 all-reduce.3.cloned.1.call-start
  36.5 0.0 copy-done.4
  36.5 0.6 dynamic-slice
  37.8 8.8 %fusion.7 = (f32[900,512]{1,0:T(8,128)S(1)}, f32[900,512]{1,0:T(8,128)}) fusion(s32[900]{0:T(1024)S(1)} %iota_add_fusion), kind=kLoop, calls=%fused_computation.12 | loop fusion | flops 4147200 | bytes 3690000 | tf_op jit(solution)/shard_map/cos | solution.py:29
  46.6 35.3 %all-to-all-done = f32[3,8,24,7,128]{4,2,3,0,1:T(8,128)} async-done(((f32[3,8,24,7,128]{4,2,3,0,1:T(8,128)}), f32[3,8,24,7,128]{4,2,3,0,1:T(8,128)}, u32[]{:S(2)}, u32[]{:S(2)}) %all-to-all-start) | async-done | bytes 2064416 | tf_op jit(solution)/shard_map/all_to_all | solution.py:80
  81.9 1.8 copy.38
  83.7 0.2 fusion.17
  83.9 0.9 fusion.10
  84.8 0.1 copy.52
  84.9 0.3 reshape.113
  85.2 0.0 copy-start.1
  85.2 0.0 copy-start.3
  85.2 4.7 %fusion.1 = f32[6,16,1024]{2,1,0:T(8,128)} fusion(f32[6,16,900]{2,1,0:T(8,128)S(1)} %reshape.113, f32[900,512]{1,0:T(8,128)} %get-tuple-element.6, f32[900,512]{1,0:T(8,128)S(1)} %get-tuple-element.5), kind=kOutput, calls=%fused_computation.3 | convolution fusion | flops 1062604800 | bytes 4425216 | tf_op jit(solution)/shard_map/dot_general | solution.py:96
  89.9 0.0 copy-done.1
  89.9 0.0 all-reduce.3.cloned.1.call-update
  90.0 0.0 copy-done.3
  90.0 0.1 compare_select_fusion
  90.0 73.0 %all-reduce.3.cloned.1.call-done = f32[6,16,1024]{2,1,0:T(8,128)} async-done(((f32[6,16,1024]{2,1,0:T(8,128)}), f32[6,16,1024]{2,1,0:T(8,128)}) %all-reduce.3.cloned.1.call-update) | async-done | bytes 393232
  163.1 0.9 dynamic-slice_multiply_fusion
  164.1 31.7 %all_gather.3 = f32[6,16,1024]{2,0,1:T(8,128)S(1)} all-gather(f32[6,2,1024]{2,0,1:T(8,128)S(1)} %copy.41), channel_id=1, replica_groups=mesh['band'=4,'col'=8] {'col'}, dimensions={1}, use_global_device_ids=true | all-gather | bytes 442368 | tf_op jit(solution)/shard_map/all_gather | solution.py:105
  195.7 5.7 %fusion = f32[6,16,900]{2,1,0:T(8,128)} fusion(f32[900,512]{1,0:T(8,128)} %get-tuple-element.6, f32[900,512]{1,0:T(8,128)S(1)} %get-tuple-element.5, f32[6,16,1024]{2,0,1:T(8,128)S(1)} %all_gather.3), kind=kOutput, calls=%fused_computation.2 | convolution fusion | flops 1062604800 | bytes 4425216 | tf_op jit(solution)/shard_map/dot_general | solution.py:106
  (6 shorter events, 0.1 us)
Async XLA Ops:
  7.2 3.1 %copy-start = (bf16[6,16384]{1,0:T(8,128)(2,1)S(1)}, bf16[6,16384]{1,0:T(8,128)(2,1)}, u32[]{:S(2)}) copy-start(bf16[6,16384]{1,0:T(8,128)(2,1)} %param.6) | copy-start | bytes 589828
  16.1 0.7 copy-start.2
  18.4 4.9 %collective-permute-start = (f32[1,8,24,7,128]{4,2,3,1,0:T(8,128)S(1)}, f32[1,8,24,7,128]{4,2,3,1,0:T(8,128)}, u32[]{:S(2)}, u32[]{:S(2)}) collective-permute-start(f32[1,8,24,7,128]{4,2,3,1,0:T(8,128)S(1)} %copy.33), channel_id=1, source_target_pairs={{0,8},{8,16},{16,24},{1,9},{9,17},{17,25},{2,10},{10,18},{18,26},{... | collective-permute-start | bytes 2064392 | tf_op jit(solution)/shard_map/ppermute | solution.py:18
  21.9 5.5 %collective-permute-start.1 = (f32[1,8,24,7,128]{4,2,3,1,0:T(8,128)S(1)}, f32[1,8,24,7,128]{4,2,3,1,0:T(8,128)}, u32[]{:S(2)}, u32[]{:S(2)}) collective-permute-start(f32[1,8,24,7,128]{4,2,3,1,0:T(8,128)S(1)} %copy.34), channel_id=1, source_target_pairs={{8,0},{16,8},{24,16},{9,1},{17,9},{25,17},{10,2},{18,10},{26,18},{... | collective-permute-start | bytes 2064392 | tf_op jit(solution)/shard_map/ppermute | solution.py:19
  30.5 6.0 %copy-start.4 = (u32[32]{0:T(128)S(1)}, u32[32]{0:T(128)}, u32[]{:S(2)}) copy-start(u32[32]{0:T(128)} %constant.84) | copy-start | bytes 388
  30.5 51.4 %all-to-all-start = ((f32[3,8,24,7,128]{4,2,3,0,1:T(8,128)}), f32[3,8,24,7,128]{4,2,3,0,1:T(8,128)}, u32[]{:S(2)}, u32[]{:S(2)}) async-start(f32[3,8,24,7,128]{4,2,3,0,1:T(8,128)} %copy.37), calls=%async_computation | async-start | bytes 4128768 | tf_op jit(solution)/shard_map/all_to_all | solution.py:80
  36.4 126.6 %all-reduce.3.cloned.1.call-start = ((), (), s32[]{:S(2)}) async-start(), calls=%async_computation.1 | async-start | bytes 786432
  85.2 4.7 %copy-start.1 = (f32[6,16,900]{2,1,0:T(8,128)}, f32[6,16,900]{2,1,0:T(8,128)S(1)}, u32[]{:S(2)}) copy-start(f32[6,16,900]{2,1,0:T(8,128)S(1)} %reshape.113) | copy-start | bytes 1036804
  85.2 4.7 %copy-start.3 = (s32[2]{0:T(128)S(1)}, s32[2]{0:T(128)}, u32[]{:S(2)}) copy-start(s32[2]{0:T(128)} %param.11) | copy-start | bytes 28
Sparse Core Ops, SparseCore 0:
  90.1 72.9 all-reduce.2
where the time goes:
time: 209 us; the launch traced here: 208 us
  waiting for transfers between devices  111 us (53%)
  blocking collectives  31.7 us (15%)
  matrix products  17.2 us (8%)
  between operations  14.9 us (7%)
  other arithmetic  13.6 us (7%)
  starting transfers between devices  10.5 us (5%)
  local copies, waits for them, and re-layouts  9.29 us (4%)
    unnamed x2, waiting for transfers between devices  73.1 us
    all_to_all x1, waiting for transfers between devices, local(): lax.all_to_all(arranged, 'col', split_axis=1, concat_axis=1, tiled=True)  35.3 us
    all_gather x1, blocking collectives, local(): band_spectra = lax.all_gather(spectrum, 'col', axis=1, tiled=True)  31.7 us
    cos x1, other arithmetic, zonal_table(): return jnp.concatenate([jnp.cos(angles), jnp.sin(angles)], axis=1)  8.82 us
    all_to_all x1, starting transfers between devices, local(): lax.all_to_all(arranged, 'col', split_axis=1, concat_axis=1, tiled=True)  5.94 us
    dot_general x1, matrix products, local(): jnp.dot(band_spectra.reshape(levels * lat_band, 2 * KW), local_table.T, p...  5.74 us
    dot_general x1, matrix products, local(): jnp.einsum('lnb,nbt->nlt', picked, weights, preferred_element_type=jnp.fl...  4.73 us
    dot_general x1, matrix products, local(): jnp.dot(remapped.reshape(levels * lat_band, longitudes_here), local_table...  4.67 us
  transfers between devices with their start and end apart: 4, of which 3 were waited for; matrix products, arithmetic and copies ran while one was open for 5% of the time, Pallas kernels for 0%

commit v1 on v0

--- a/solution.py
+++ b/solution.py
@@ -102,7 +102,8 @@
     partial_spectra = partial_spectra.reshape(levels, lat_band, 2 * KW)
     spectrum = lax.psum_scatter(partial_spectra, "col", scatter_dimension=1, tiled=True)
     spectrum = spectrum * retained[None]
-    band_spectra = lax.all_gather(spectrum, "col", axis=1, tiled=True)
+    tiles = lax.all_gather(spectrum, "col")
+    band_spectra = jnp.concatenate(tiles, axis=1)
     filtered = jnp.dot(
         band_spectra.reshape(levels * lat_band, 2 * KW),
         local_table.T,

time: 209 us -> 209 us (level)
  no operation moved by 1% of the time
where the time goes in v1:
time: 209 us; the launch traced here: 208 us
  waiting for transfers between devices  111 us (53%)
  blocking collectives  31.4 us (15%)
  matrix products  17.1 us (8%)
  between operations  14.9 us (7%)
  other arithmetic  13.6 us (7%)
  starting transfers between devices  10.5 us (5%)
  local copies, waits for them, and re-layouts  9.57 us (5%)
    unnamed x2, waiting for transfers between devices  73 us
    all_to_all x1, waiting for transfers between devices, local(): lax.all_to_all(arranged, 'col', split_axis=1, concat_axis=1, tiled=True)  35.3 us
    all_gather x1, blocking collectives, local(): tiles = lax.all_gather(spectrum, 'col')  31.4 us
    cos x1, other arithmetic, zonal_table(): return jnp.concatenate([jnp.cos(angles), jnp.sin(angles)], axis=1)  8.82 us
    all_to_all x1, starting transfers between devices, local(): lax.all_to_all(arranged, 'col', split_axis=1, concat_axis=1, tiled=True)  5.94 us
    dot_general x1, matrix products, local(): jnp.dot(band_spectra.reshape(levels * lat_band, 2 * KW), local_table.T, p...  5.64 us
    dot_general x1, matrix products, local(): jnp.einsum('lnb,nbt->nlt', picked, weights, preferred_element_type=jnp.fl...  4.73 us
    dot_general x1, matrix products, local(): jnp.dot(remapped.reshape(levels * lat_band, longitudes_here), local_table...  4.67 us
  transfers between devices with their start and end apart: 4, of which 3 were waited for; matrix products, arithmetic and copies ran while one was open for 5% of the time, Pallas kernels for 0%

profile of v1, /device:TPU:0, one launch (start us, length us, event | category | flops | bytes accessed | tf_op | source)
XLA Modules:
  0.0 208.2 jit_solution(5660498746091327981)
XLA Ops:
  7.2 0.0 copy-start
  7.2 0.7 compare_select_fusion.1
  7.9 0.7 compare_and_fusion
  8.6 0.9 convert_reduce_fusion
  9.5 0.7 convert_element_type.22
  10.2 0.0 copy-done
  10.2 0.8 gather_fusion
  11.0 4.7 %fusion.12 = f32[256,6,128]{2,1,0:T(8,128)S(1)} fusion(bf16[256,128,128]{2,1,0:T(8,128)(2,1)} %param.7, bf16[256,6,128]{2,1,0:T(8,128)(2,1)S(1)} %gather_fusion, pred[256]{0:T(512)(128)(4,1)S(1)} %compare_and_fusion), kind=kOutput, calls=%fused_computation.20 | convolution fusion | flops 50528256 | bytes 9568512 | tf_op jit(solution)/shard_map/lnb,nbt->nlt/dot_general | solution.py:56
  15.8 0.3 broadcast_in_dim.37
  16.1 0.0 copy-start.2
  16.1 0.2 pad_maximum_fusion.1
  16.4 0.4 copy.32
  16.7 0.1 copy-done.2
  16.8 1.2 fusion.11
  18.0 0.1 fusion.28
  18.2 0.1 slice.28
  18.3 0.1 copy.33
  18.4 3.3 %collective-permute-start = (f32[1,8,24,7,128]{4,2,3,1,0:T(8,128)S(1)}, f32[1,8,24,7,128]{4,2,3,1,0:T(8,128)}, u32[]{:S(2)}, u32[]{:S(2)}) collective-permute-start(f32[1,8,24,7,128]{4,2,3,1,0:T(8,128)S(1)} %copy.33), channel_id=1, source_target_pairs={{0,8},{8,16},{16,24},{1,9},{9,17},{17,25},{2,10},{10,18},{18,26},{... | collective-permute-start | bytes 2064392 | tf_op jit(solution)/shard_map/ppermute | solution.py:18
  21.7 0.1 slice.32
  21.8 0.1 copy.34
  21.9 1.3 collective-permute-start.1
  23.2 0.1 slice.30
  23.3 0.0 collective-permute-done
  23.3 1.2 copy.35
  24.6 2.8 %collective-permute-done.1 = f32[1,8,24,7,128]{4,2,3,1,0:T(8,128)} collective-permute-done((f32[1,8,24,7,128]{4,2,3,1,0:T(8,128)S(1)}, f32[1,8,24,7,128]{4,2,3,1,0:T(8,128)}, u32[]{:S(2)}, u32[]{:S(2)}) %collective-permute-start.1) | collective-permute-done | bytes 688160 | tf_op jit(solution)/shard_map/ppermute | solution.py:19
  27.4 1.2 copy.36
  28.6 0.2 pad_maximum_fusion
  28.9 1.7 copy.37
  30.5 0.0 copy-start.4
  30.5 5.9 %all-to-all-start = ((f32[3,8,24,7,128]{4,2,3,0,1:T(8,128)}), f32[3,8,24,7,128]{4,2,3,0,1:T(8,128)}, u32[]{:S(2)}, u32[]{:S(2)}) async-start(f32[3,8,24,7,128]{4,2,3,0,1:T(8,128)} %copy.37), calls=%async_computation | async-start | bytes 4128768 | tf_op jit(solution)/shard_map/all_to_all | solution.py:80
  36.4 0.0 all-reduce.3.cloned.1.call-start
  36.5 0.0 copy-done.4
  36.5 0.6 dynamic-slice
  37.8 8.8 %fusion.7 = (f32[900,512]{1,0:T(8,128)S(1)}, f32[900,512]{1,0:T(8,128)}) fusion(s32[900]{0:T(1024)S(1)} %iota_add_fusion), kind=kLoop, calls=%fused_computation.12 | loop fusion | flops 4147200 | bytes 3690000 | tf_op jit(solution)/shard_map/cos | solution.py:29
  46.6 35.3 %all-to-all-done = f32[3,8,24,7,128]{4,2,3,0,1:T(8,128)} async-done(((f32[3,8,24,7,128]{4,2,3,0,1:T(8,128)}), f32[3,8,24,7,128]{4,2,3,0,1:T(8,128)}, u32[]{:S(2)}, u32[]{:S(2)}) %all-to-all-start) | async-done | bytes 2064416 | tf_op jit(solution)/shard_map/all_to_all | solution.py:80
  81.9 1.8 copy.38
  83.7 0.2 fusion.16
  83.9 0.9 fusion.10
  84.8 0.1 copy.50
  84.9 0.3 reshape.115
  85.2 0.0 copy-start.1
  85.2 0.0 copy-start.3
  85.2 4.7 %fusion.1 = f32[6,16,1024]{2,1,0:T(8,128)} fusion(f32[6,16,900]{2,1,0:T(8,128)S(1)} %reshape.115, f32[900,512]{1,0:T(8,128)} %get-tuple-element.6, f32[900,512]{1,0:T(8,128)S(1)} %get-tuple-element.5), kind=kOutput, calls=%fused_computation.3 | convolution fusion | flops 1062604800 | bytes 4425216 | tf_op jit(solution)/shard_map/dot_general | solution.py:96
  89.9 0.0 copy-done.1
  89.9 0.0 all-reduce.3.cloned.1.call-update
  90.0 0.0 copy-done.3
  90.0 0.1 compare_select_fusion
  90.0 73.0 %all-reduce.3.cloned.1.call-done = f32[6,16,1024]{2,1,0:T(8,128)} async-done(((f32[6,16,1024]{2,1,0:T(8,128)}), f32[6,16,1024]{2,1,0:T(8,128)}) %all-reduce.3.cloned.1.call-update) | async-done | bytes 393232
  163.1 0.9 dynamic-slice_multiply_fusion
  164.0 31.4 %all-gather = f32[48,2,1024]{2,1,0:T(2,128)S(1)} all-gather(f32[6,2,1024]{2,1,0:T(2,128)S(1)} %dynamic-slice_multiply_fusion), channel_id=2, replica_groups=mesh['band'=4,'col'=8] {'col'}, dimensions={0}, use_global_device_ids=true | all-gather | bytes 442368 | tf_op jit(solution)/shard_map/all_gather | solution.py:105
  195.5 0.3 dot_general.27
  195.8 5.6 %fusion = f32[6,16,900]{2,1,0:T(8,128)} fusion(f32[6,16,1024]{2,1,0:T(8,128)S(1)} %dot_general.27, f32[900,512]{1,0:T(8,128)} %get-tuple-element.6, f32[900,512]{1,0:T(8,128)S(1)} %get-tuple-element.5), kind=kOutput, calls=%fused_computation.2 | convolution fusion | flops 1062604800 | bytes 4425216 | tf_op jit(solution)/shard_map/dot_general | solution.py:107
  (6 shorter events, 0.1 us)
Async XLA Ops:
  7.2 3.1 %copy-start = (bf16[6,16384]{1,0:T(8,128)(2,1)S(1)}, bf16[6,16384]{1,0:T(8,128)(2,1)}, u32[]{:S(2)}) copy-start(bf16[6,16384]{1,0:T(8,128)(2,1)} %param.6) | copy-start | bytes 589828
  16.1 0.7 copy-start.2
  18.4 4.9 %collective-permute-start = (f32[1,8,24,7,128]{4,2,3,1,0:T(8,128)S(1)}, f32[1,8,24,7,128]{4,2,3,1,0:T(8,128)}, u32[]{:S(2)}, u32[]{:S(2)}) collective-permute-start(f32[1,8,24,7,128]{4,2,3,1,0:T(8,128)S(1)} %copy.33), channel_id=1, source_target_pairs={{0,8},{8,16},{16,24},{1,9},{9,17},{17,25},{2,10},{10,18},{18,26},{... | collective-permute-start | bytes 2064392 | tf_op jit(solution)/shard_map/ppermute | solution.py:18
  21.9 5.5 %collective-permute-start.1 = (f32[1,8,24,7,128]{4,2,3,1,0:T(8,128)S(1)}, f32[1,8,24,7,128]{4,2,3,1,0:T(8,128)}, u32[]{:S(2)}, u32[]{:S(2)}) collective-permute-start(f32[1,8,24,7,128]{4,2,3,1,0:T(8,128)S(1)} %copy.34), channel_id=1, source_target_pairs={{8,0},{16,8},{24,16},{9,1},{17,9},{25,17},{10,2},{18,10},{26,18},{... | collective-permute-start | bytes 2064392 | tf_op jit(solution)/shard_map/ppermute | solution.py:19
  30.5 6.0 %copy-start.4 = (u32[32]{0:T(128)S(1)}, u32[32]{0:T(128)}, u32[]{:S(2)}) copy-start(u32[32]{0:T(128)} %constant.84) | copy-start | bytes 388
  30.5 51.4 %all-to-all-start = ((f32[3,8,24,7,128]{4,2,3,0,1:T(8,128)}), f32[3,8,24,7,128]{4,2,3,0,1:T(8,128)}, u32[]{:S(2)}, u32[]{:S(2)}) async-start(f32[3,8,24,7,128]{4,2,3,0,1:T(8,128)} %copy.37), calls=%async_computation | async-start | bytes 4128768 | tf_op jit(solution)/shard_map/all_to_all | solution.py:80
  36.4 126.6 %all-reduce.3.cloned.1.call-start = ((), (), s32[]{:S(2)}) async-start(), calls=%async_computation.1 | async-start | bytes 786432
  85.2 4.7 %copy-start.1 = (f32[6,16,900]{2,1,0:T(8,128)}, f32[6,16,900]{2,1,0:T(8,128)S(1)}, u32[]{:S(2)}) copy-start(f32[6,16,900]{2,1,0:T(8,128)S(1)} %reshape.115) | copy-start | bytes 1036804
  85.2 4.7 %copy-start.3 = (s32[2]{0:T(128)S(1)}, s32[2]{0:T(128)}, u32[]{:S(2)}) copy-start(s32[2]{0:T(128)} %param.11) | copy-start | bytes 28
Sparse Core Ops, SparseCore 0:
  90.1 72.9 all-reduce.2
